TPU v7x, 32 devices: a whole 2x2x4 slice. The times are simulated.
32 devices in a mesh: dp: 8 (over z, core), fsdp: 4 (over y, x).
Axes of the slice: x: 2, y: 2, z: 4, core: 2. Of those that a mesh axis runs over, the one named last changes fastest.
Arguments:
- logits: bfloat16 [4096, 32000], P('dp', 'fsdp'), may hold values from -115 to 125
- labels: int32 [4096], P('dp'), may hold values from 0 to 31999
- activations: bfloat16 [4096, 5120], P('dp', 'fsdp'), may hold values from -6 to 6
- proj_in: bfloat16 [5120, 64], P('fsdp'), may hold values from -0.078125 to 0.078125
- proj_out: bfloat16 [32000, 64], P('fsdp'), may hold values from -6 to 6
Outputs:
- features: float32 [512, 4096], P(('dp', 'fsdp'))
- gram: float32 [4096, 4096], P('fsdp', 'dp')
All inputs are finite; a program needn't handle non-finite values.
Results may differ from a plain program's by a relative error of at most 0.014.
Values may be sent and summed in bfloat16 or wider, within the bound.
No kernel may reach another device: no remote copies, remote signals or barrier semaphores. Data moves between devices by JAX's collectives and lax.ppermute only.
A program may use at most 64 MiB of HBM per device.

v0:
```python
import jax
import jax.numpy as jnp
from jax import lax
from jax.sharding import PartitionSpec as P

SEQ = 8


def body(logits, labels, activations, proj_in, proj_out):
    vocab_local = logits.shape[1]
    values = logits.astype(jnp.float32)
    local_top = jnp.max(values, axis=1)
    row_top = lax.pmax(local_top, "fsdp")
    row_sum = lax.psum(jnp.sum(jnp.exp(values - row_top[:, None]), axis=1), "fsdp")
    prob = jnp.exp(values - row_top[:, None]) / row_sum[:, None]
    columns = lax.axis_index("fsdp") * vocab_local + lax.broadcasted_iota(
        jnp.int32, (1, vocab_local), 1
    )
    onehot = (columns == labels[:, None]).astype(jnp.float32)
    errors = (prob - onehot).astype(jnp.bfloat16)
    part_left = jnp.dot(activations, proj_in, preferred_element_type=jnp.float32)
    part_right = jnp.dot(errors, proj_out, preferred_element_type=jnp.float32)
    left, right = (
        lax.psum_scatter(part_left, "fsdp", scatter_dimension=0, tiled=True),
        lax.psum_scatter(part_right, "fsdp", scatter_dimension=0, tiled=True),
    )
    count = left.shape[0] // SEQ
    width_in = proj_in.shape[1]
    width_out = proj_out.shape[1]
    sketch = jnp.einsum(
        "esi,esj->eij", left.reshape(count, SEQ, width_in), right.reshape(count, SEQ, width_out)
    )
    features = sketch.reshape(count, width_in * width_out)
    rounded = features.astype(jnp.bfloat16)
    feat_all = features.shape[1]
    gram_rows = feat_all // lax.axis_size("fsdp")
    row_start = lax.axis_index("fsdp") * gram_rows
    folded = lax.all_gather(rounded, "fsdp", axis=0, tiled=True)
    column_share = lax.all_to_all(folded, "dp", split_axis=1, concat_axis=0, tiled=True)
    row_share = lax.dynamic_slice_in_dim(folded, row_start, gram_rows, 1)
    gram = lax.dot_general(
        lax.all_gather(row_share, "dp", axis=0, tiled=True),
        column_share,
        (((0,), (0,)), ((), ())),
        preferred_element_type=jnp.float32,
    )
    return (features, gram)


def solution(mesh):
    in_specs = (P("dp", "fsdp"), P("dp"), P("dp", "fsdp"), P("fsdp", None), P("fsdp", None))
    out_specs = (P(("dp", "fsdp"), None), P("fsdp", "dp"))
    return jax.shard_map(body, mesh=mesh, in_specs=in_specs, out_specs=out_specs, check_vma=False)
```

profile of v0, /device:TPU:0, one launch (start us, length us, event | category | flops | bytes accessed | tf_op | source)
XLA Modules:
  0.0 152.0 jit_solution(3357230668672112707)
XLA Ops:
  7.2 0.0 copy-start
  7.2 0.0 reduce-scatter.5.cloned.1.call-start
  7.2 0.0 copy-start.3
  7.2 0.0 copy-start.4
  7.2 4.6 %reduce_max.14 = bf16[512]{0:T(512)(128)(2,1)S(1)} reduce(bf16[512,8000]{0,1:T(8,128)(2,1)} %param.5, bf16[]{:T(256)} %constant.7.clone.1), dimensions={1}, to_apply=%region_1.0 | reduce | flops 4095488 | bytes 8193026 | tf_op jit(solution)/shard_map/reduce_max | solution.py:12
  11.9 11.4 %pmax.7 = f32[512]{0:T(512)S(1)} all-reduce(bf16[512]{0:T(512)(128)(2,1)S(1)} %reduce_max.14), channel_id=1, replica_groups=mesh['dp'=8,'fsdp'=4] {'fsdp'}, use_global_device_ids=true, to_apply=%region_2.0 | all-reduce | flops 512 | bytes 3072 | tf_op jit(solution)/shard_map/pmax | solution.py:13
  23.2 6.1 %fusion = f32[512]{0:T(512)S(1)} fusion(bf16[512,8000]{0,1:T(8,128)(2,1)} %param.5, f32[512]{0:T(512)S(1)} %pmax.7), kind=kLoop, calls=%fused_computation.2 | loop fusion | flops 12287488 | bytes 8196096 | tf_op jit(solution)/shard_map/reduce_sum | solution.py:14
  29.3 8.0 %psum.7 = f32[512]{0:T(512)S(1)} all-reduce(f32[512]{0:T(512)S(1)} %fusion), channel_id=1, replica_groups=mesh['dp'=8,'fsdp'=4] {'fsdp'}, use_global_device_ids=true, to_apply=%region_4.0 | all-reduce | flops 512 | bytes 4096 | tf_op jit(solution)/shard_map/psum | solution.py:14
  37.3 0.0 copy-done.3
  37.3 0.0 copy-done.4
  37.3 0.0 copy-start.2
  37.3 10.7 %fusion.1 = f32[512,64]{0,1:T(8,128)} fusion(bf16[8000,64]{0,1:T(8,128)(2,1)S(1)} %copy-done.3, bf16[512,8000]{0,1:T(8,128)(2,1)} %param.5, s32[512]{0:T(512)S(1)} %copy-done.4, f32[512]{0:T(512)S(1)} %psum.7, f32[512]{0:T(512)S(1)} %pmax.7, s32[8000]{0:T(1024)S(1)} %iota_add_fusion), kind=kOutput, calls=%fused_computation.3 | convolution fusion | flops 552960000 | bytes 9385216 | tf_op jit(solution)/shard_map/dot_general | solution.py:22
  48.0 0.0 reduce-scatter.5.cloned.1.call-update
  48.0 0.0 reduce-scatter.3.cloned.1.call-start
  48.1 0.0 copy-done
  48.1 0.0 copy-done.2
  48.1 1.2 fusion.5
  49.3 0.0 reduce-scatter.3.cloned.1.call-update
  49.3 0.0 all-gather.2.cloned.1.call-start
  49.3 23.3 %reduce-scatter.5.cloned.1.call-done = f32[128,64]{0,1:T(8,128)} async-done(((f32[512,64]{0,1:T(8,128)}), f32[128,64]{0,1:T(8,128)}) %reduce-scatter.5.cloned.1.call-update) | async-done | bytes 32784 | tf_op jit(solution)/shard_map/reduce_scatter | solution.py:25
  72.6 0.9 copy.15
  73.5 26.6 %reduce-scatter.3.cloned.1.call-done = f32[128,64]{0,1:T(8,128)} async-done(((f32[512,64]{0,1:T(8,128)}), f32[128,64]{0,1:T(8,128)}) %reduce-scatter.3.cloned.1.call-update) | async-done | bytes 32784 | tf_op jit(solution)/shard_map/reduce_scatter | solution.py:24
  100.1 0.9 copy.14
  101.0 0.3 fusion.2
  101.3 0.2 reshape.26
  101.5 0.0 copy-start.1
  101.5 10.5 %all_gather.6 = bf16[64,4096]{1,0:T(8,128)(2,1)S(1)} all-gather(bf16[16,4096]{1,0:T(8,128)(2,1)S(1)} %convert_element_type.15), channel_id=1, replica_groups=mesh['dp'=8,'fsdp'=4] {'fsdp'}, dimensions={0}, use_global_device_ids=true | all-gather | bytes 655360 | tf_op jit(solution)/shard_map/all_gather | solution.py:38
  112.0 0.7 constant_dynamic-slice_fusion
  112.6 0.0 all-gather.2.cloned.1.call-update
  112.7 28.1 %all_to_all.19 = bf16[64,8,512]{2,0,1:T(8,128)(2,1)S(1)} all-to-all(bf16[64,8,512]{2,0,1:T(8,128)(2,1)S(1)} %bitcast.20), channel_id=1, replica_groups=mesh['dp'=8,'fsdp'=4] {'dp'}, dimensions={1} | all-to-all | bytes 1048576 | tf_op jit(solution)/shard_map/all_to_all | solution.py:39
  140.9 1.4 all-gather.2.cloned.1.call-done
  142.2 3.3 %fusion.6 = f32[1024,512]{1,0:T(8,128)} fusion(bf16[512,1024]{1,0:T(8,128)(2,1)} %all-gather.2.cloned.1.call-done, bf16[512,512]{1,0:T(8,128)(2,1)S(1)} %bitcast.19), kind=kOutput, calls=%fused_computation.11 | convolution fusion | flops 536870912 | bytes 3670016 | tf_op jit(solution)/shard_map/dot_general | solution.py:41
  145.5 0.0 copy-done.1
  (3 shorter events, 0.1 us)
Async XLA Ops:
  7.2 40.9 %copy-start = (bf16[512,1280]{1,0:T(8,128)(2,1)S(1)}, bf16[512,1280]{1,0:T(8,128)(2,1)}, u32[]{:S(2)}) copy-start(bf16[512,1280]{1,0:T(8,128)(2,1)} %param.7) | copy-start | bytes 3932164
  7.2 65.4 %reduce-scatter.5.cloned.1.call-start = ((), (), s32[]{:S(2)}) async-start(), calls=%async_computation.4 | async-start | bytes 163840 | tf_op jit(solution)/shard_map/reduce_scatter | solution.py:25
  7.2 30.1 %copy-start.3 = (bf16[8000,64]{0,1:T(8,128)(2,1)S(1)}, bf16[8000,64]{0,1:T(8,128)(2,1)}, u32[]{:S(2)}) copy-start(bf16[8000,64]{0,1:T(8,128)(2,1)} %param.9) | copy-start | bytes 3072004
  7.2 30.1 %copy-start.4 = (s32[512]{0:T(512)S(1)}, s32[512]{0:T(512)}, u32[]{:S(2)}) copy-start(s32[512]{0:T(512)} %param.6) | copy-start | bytes 6148
  37.3 10.8 %copy-start.2 = (bf16[1280,64]{0,1:T(8,128)(2,1)S(1)}, bf16[1280,64]{0,1:T(8,128)(2,1)}, u32[]{:S(2)}) copy-start(bf16[1280,64]{0,1:T(8,128)(2,1)} %param.8) | copy-start | bytes 491524
  48.0 52.1 %reduce-scatter.3.cloned.1.call-start = ((), (), s32[]{:S(2)}) async-start(), calls=%async_computation.3 | async-start | bytes 163840 | tf_op jit(solution)/shard_map/reduce_scatter | solution.py:24
  49.3 92.9 %all-gather.2.cloned.1.call-start = ((), (), s32[]{:S(2)}) async-start(), calls=%async_computation.5 | async-start | bytes 1179648 | tf_op jit(solution)/shard_map/all_gather | solution.py:42
  101.5 44.0 %copy-start.1 = (f32[16,4096]{1,0:T(8,128)}, f32[16,4096]{1,0:T(8,128)S(1)}, u32[]{:S(2)}) copy-start(f32[16,4096]{1,0:T(8,128)S(1)} %reshape.26) | copy-start | bytes 786436
Sparse Core Ops, SparseCore 0:
  48.1 24.4 reduce-scatter.4
  75.9 24.1 reduce-scatter.2
  112.8 29.3 all-gather.1
where the time goes:
time: 153 us; the launch traced here: 152 us
  blocking collectives  58 us (38%)
  waiting for transfers between devices  51.3 us (34%)
  matrix products  15.4 us (10%)
  between operations  13.8 us (9%)
  other arithmetic  10.7 us (7%)
  local copies, waits for them, and re-layouts  2.64 us (2%)
    all_to_all x1, blocking collectives, body(): lax.all_to_all(folded, 'dp', split_axis=1, concat_axis=0, tiled=True)  28.1 us
    reduce_scatter x1, waiting for transfers between devices, body(): lax.psum_scatter(part_left, 'fsdp', scatter_dimension=0, tiled=True)  26.6 us
    reduce_scatter x1, waiting for transfers between devices, body(): lax.psum_scatter(part_right, 'fsdp', scatter_dimension=0, tiled=True)  23.3 us
    pmax x1, blocking collectives, body(): row_top = lax.pmax(local_top, 'fsdp')  11.4 us
    dot_general x1, matrix products, body(): part_right = jnp.dot(errors, proj_out, preferred_element_type=jnp.float32)  10.7 us
    all_gather x1, blocking collectives, body(): folded = lax.all_gather(rounded, 'fsdp', axis=0, tiled=True)  10.5 us
    psum x1, blocking collectives, body(): lax.psum(jnp.sum(jnp.exp(values - row_top[:, None]), axis=1), 'fsdp')  7.98 us
    reduce_sum x1, other arithmetic, body(): jnp.sum(jnp.exp(values - row_top[:, None]), axis=1)  6.09 us
  transfers between devices with their start and end apart: 3, of which 3 were waited for; matrix products, arithmetic and copies ran while one was open for 1% of the time, Pallas kernels for 0%

commit v1 on v0

--- a/solution.py
+++ b/solution.py
@@ -35,7 +35,13 @@
     feat_all = features.shape[1]
     gram_rows = feat_all // lax.axis_size("fsdp")
     row_start = lax.axis_index("fsdp") * gram_rows
-    folded = lax.all_gather(rounded, "fsdp", axis=0, tiled=True)
+    size = lax.axis_size("fsdp")
+    current, blocks = (rounded, [rounded])
+    for _ in range(size - 1):
+        current = lax.ppermute(current, "fsdp", [(i, (i + 1) % size) for i in range(size)])
+        blocks.insert(0, current)
+    flat = jnp.concatenate(blocks, axis=0)
+    folded = jnp.roll(flat, (lax.axis_index("fsdp") + 1) * rounded.shape[0], axis=0)
     column_share = lax.all_to_all(folded, "dp", split_axis=1, concat_axis=0, tiled=True)
     row_share = lax.dynamic_slice_in_dim(folded, row_start, gram_rows, 1)
     gram = lax.dot_general(

time: 153 us -> 160 us (1.046)
  waiting for transfers between devices: 51.3 us -> 66.8 us
  blocking collectives: 58 us -> 47.5 us
  starting transfers between devices: 0.12 us -> 2.24 us
    ppermute x0 -> x3, waiting for transfers between devices: none -> 15.5 us  [body(): lax.ppermute(current, 'fsdp', [(i, (i + 1) % size) for i in range(size)])]
    all_gather x1 -> x0, blocking collectives: 10.5 us -> none  [body(): folded = lax.all_gather(rounded, 'fsdp', axis=0, tiled=True)]
    ppermute x0 -> x3, starting transfers between devices: none -> 2.12 us  [body(): lax.ppermute(current, 'fsdp', [(i, (i + 1) % size) for i in range(size)])]
  transfers between devices with their start and end apart: 3 -> 6, of which waited for: 3 -> 6; matrix products, arithmetic and copies ran while one was open for 1% -> 1% of each run, Pallas kernels for 0% -> 0%
where the time goes in v1:
time: 160 us
  waiting for transfers between devices  66.8 us (42%)
  blocking collectives  47.5 us (30%)
  matrix products  15.4 us (10%)
  between operations  13.9 us (9%)
  other arithmetic  10.7 us (7%)
  local copies, waits for them, and re-layouts  2.87 us (2%)
  starting transfers between devices  2.24 us (1%)
    all_to_all x1, blocking collectives, body(): lax.all_to_all(folded, 'dp', split_axis=1, concat_axis=0, tiled=True)  28.2 us
    reduce_scatter x1, waiting for transfers between devices, body(): lax.psum_scatter(part_left, 'fsdp', scatter_dimension=0, tiled=True)  26.6 us
    reduce_scatter x1, waiting for transfers between devices, body(): lax.psum_scatter(part_right, 'fsdp', scatter_dimension=0, tiled=True)  23.3 us
    ppermute x3, waiting for transfers between devices, body(): lax.ppermute(current, 'fsdp', [(i, (i + 1) % size) for i in range(size)])  15.5 us
    pmax x1, blocking collectives, body(): row_top = lax.pmax(local_top, 'fsdp')  11.4 us
    dot_general x1, matrix products, body(): part_right = jnp.dot(errors, proj_out, preferred_element_type=jnp.float32)  10.7 us
    psum x1, blocking collectives, body(): lax.psum(jnp.sum(jnp.exp(values - row_top[:, None]), axis=1), 'fsdp')  7.98 us
    reduce_sum x1, other arithmetic, body(): jnp.sum(jnp.exp(values - row_top[:, None]), axis=1)  6.09 us
  transfers between devices with their start and end apart: 6, of which 6 were waited for; matrix products, arithmetic and copies ran while one was open for 1% of the time, Pallas kernels for 0%

profile of v1, /device:TPU:0, one launch (start us, length us, event | category | flops | bytes accessed | tf_op | source)
XLA Modules:
  0.0 159.5 jit_solution(1890970716217967239)
XLA Ops:
  7.2 0.0 copy-start
  7.2 0.0 reduce-scatter.5.cloned.1.call-start
  7.2 0.0 copy-start.3
  7.2 0.0 copy-start.4
  7.2 4.6 %reduce_max.14 = bf16[512]{0:T(512)(128)(2,1)S(1)} reduce(bf16[512,8000]{0,1:T(8,128)(2,1)} %param.5, bf16[]{:T(256)} %constant.40.clone.1), dimensions={1}, to_apply=%region_1.0 | reduce | flops 4095488 | bytes 8193026 | tf_op jit(solution)/shard_map/reduce_max | solution.py:12
  11.9 11.4 %pmax.7 = f32[512]{0:T(512)S(1)} all-reduce(bf16[512]{0:T(512)(128)(2,1)S(1)} %reduce_max.14), channel_id=1, replica_groups=mesh['dp'=8,'fsdp'=4] {'fsdp'}, use_global_device_ids=true, to_apply=%region_2.0 | all-reduce | flops 512 | bytes 3072 | tf_op jit(solution)/shard_map/pmax | solution.py:13
  23.2 6.1 %fusion = f32[512]{0:T(512)S(1)} fusion(bf16[512,8000]{0,1:T(8,128)(2,1)} %param.5, f32[512]{0:T(512)S(1)} %pmax.7), kind=kLoop, calls=%fused_computation.2 | loop fusion | flops 12287488 | bytes 8196096 | tf_op jit(solution)/shard_map/reduce_sum | solution.py:14
  29.3 8.0 %psum.7 = f32[512]{0:T(512)S(1)} all-reduce(f32[512]{0:T(512)S(1)} %fusion), channel_id=1, replica_groups=mesh['dp'=8,'fsdp'=4] {'fsdp'}, use_global_device_ids=true, to_apply=%region_4.0 | all-reduce | flops 512 | bytes 4096 | tf_op jit(solution)/shard_map/psum | solution.py:14
  37.3 0.0 copy-done.3
  37.3 0.0 copy-done.4
  37.3 0.0 copy-start.2
  37.3 10.7 %fusion.1 = f32[512,64]{0,1:T(8,128)} fusion(bf16[8000,64]{0,1:T(8,128)(2,1)S(1)} %copy-done.3, bf16[512,8000]{0,1:T(8,128)(2,1)} %param.5, s32[512]{0:T(512)S(1)} %copy-done.4, f32[512]{0:T(512)S(1)} %psum.7, f32[512]{0:T(512)S(1)} %pmax.7, s32[8000]{0:T(1024)S(1)} %iota_add_fusion), kind=kOutput, calls=%fused_computation.3 | convolution fusion | flops 552960000 | bytes 9385216 | tf_op jit(solution)/shard_map/dot_general | solution.py:22
  48.0 0.0 reduce-scatter.5.cloned.1.call-update
  48.0 0.0 reduce-scatter.3.cloned.1.call-start
  48.1 0.0 copy-done
  48.1 0.0 copy-done.2
  48.1 1.2 fusion.5
  49.3 0.0 reduce-scatter.3.cloned.1.call-update
  49.3 0.0 all-gather.2.cloned.1.call-start
  49.3 23.3 %reduce-scatter.5.cloned.1.call-done = f32[128,64]{0,1:T(8,128)} async-done(((f32[512,64]{0,1:T(8,128)}), f32[128,64]{0,1:T(8,128)}) %reduce-scatter.5.cloned.1.call-update) | async-done | bytes 32784 | tf_op jit(solution)/shard_map/reduce_scatter | solution.py:25
  72.6 0.9 copy.15
  73.5 26.6 %reduce-scatter.3.cloned.1.call-done = f32[128,64]{0,1:T(8,128)} async-done(((f32[512,64]{0,1:T(8,128)}), f32[128,64]{0,1:T(8,128)}) %reduce-scatter.3.cloned.1.call-update) | async-done | bytes 32784 | tf_op jit(solution)/shard_map/reduce_scatter | solution.py:24
  100.1 0.9 copy.14
  101.0 0.3 fusion.2
  101.3 0.2 reshape.26
  101.5 0.0 copy-start.1
  101.5 1.5 collective-permute-start
  103.0 4.4 %collective-permute-done = bf16[16,4096]{1,0:T(8,128)(2,1)S(1)} collective-permute-done((bf16[16,4096]{1,0:T(8,128)(2,1)S(1)}, bf16[16,4096]{1,0:T(8,128)(2,1)S(1)}, u32[]{:S(2)}, u32[]{:S(2)}) %collective-permute-start) | collective-permute-done | bytes 131104 | tf_op jit(solution)/shard_map/ppermute | solution.py:41
  107.4 0.6 collective-permute-start.1
  108.0 5.3 %collective-permute-done.1 = bf16[16,4096]{1,0:T(8,128)(2,1)S(1)} collective-permute-done((bf16[16,4096]{1,0:T(8,128)(2,1)S(1)}, bf16[16,4096]{1,0:T(8,128)(2,1)S(1)}, u32[]{:S(2)}, u32[]{:S(2)}) %collective-permute-start.1) | collective-permute-done | bytes 131104 | tf_op jit(solution)/shard_map/ppermute | solution.py:41
  113.3 0.0 collective-permute-start.2
  113.3 5.9 %collective-permute-done.2 = bf16[16,4096]{1,0:T(8,128)(2,1)S(1)} collective-permute-done((bf16[16,4096]{1,0:T(8,128)(2,1)S(1)}, bf16[16,4096]{1,0:T(8,128)(2,1)S(1)}, u32[]{:S(2)}, u32[]{:S(2)}) %collective-permute-start.2) | collective-permute-done | bytes 131104 | tf_op jit(solution)/shard_map/ppermute | solution.py:41
  119.3 0.8 dynamic_slice.7
  120.1 0.0 all-gather.2.cloned.1.call-update
  120.2 28.2 %all_to_all.19 = bf16[64,8,512]{2,0,1:T(8,128)(2,1)S(1)} all-to-all(bf16[64,8,512]{2,0,1:T(8,128)(2,1)S(1)} %bitcast.20), channel_id=1, replica_groups=mesh['dp'=8,'fsdp'=4] {'dp'}, dimensions={1} | all-to-all | bytes 1048576 | tf_op jit(solution)/shard_map/all_to_all | solution.py:45
  148.4 1.4 all-gather.2.cloned.1.call-done
  149.7 3.3 %fusion.6 = f32[1024,512]{1,0:T(8,128)} fusion(bf16[512,1024]{1,0:T(8,128)(2,1)} %all-gather.2.cloned.1.call-done, bf16[512,512]{1,0:T(8,128)(2,1)S(1)} %bitcast.18), kind=kOutput, calls=%fused_computation.19 | convolution fusion | flops 536870912 | bytes 3670016 | tf_op jit(solution)/shard_map/dot_general | solution.py:47
  153.0 0.0 copy-done.1
  (12 shorter events, 0.2 us)
Async XLA Ops:
  7.2 40.9 %copy-start = (bf16[512,1280]{1,0:T(8,128)(2,1)S(1)}, bf16[512,1280]{1,0:T(8,128)(2,1)}, u32[]{:S(2)}) copy-start(bf16[512,1280]{1,0:T(8,128)(2,1)} %param.7) | copy-start | bytes 3932164
  7.2 65.4 %reduce-scatter.5.cloned.1.call-start = ((), (), s32[]{:S(2)}) async-start(), calls=%async_computation.4 | async-start | bytes 163840 | tf_op jit(solution)/shard_map/reduce_scatter | solution.py:25
  7.2 30.1 %copy-start.3 = (bf16[8000,64]{0,1:T(8,128)(2,1)S(1)}, bf16[8000,64]{0,1:T(8,128)(2,1)}, u32[]{:S(2)}) copy-start(bf16[8000,64]{0,1:T(8,128)(2,1)} %param.9) | copy-start | bytes 3072004
  7.2 30.1 %copy-start.4 = (s32[512]{0:T(512)S(1)}, s32[512]{0:T(512)}, u32[]{:S(2)}) copy-start(s32[512]{0:T(512)} %param.6) | copy-start | bytes 6148
  37.3 10.8 %copy-start.2 = (bf16[1280,64]{0,1:T(8,128)(2,1)S(1)}, bf16[1280,64]{0,1:T(8,128)(2,1)}, u32[]{:S(2)}) copy-start(bf16[1280,64]{0,1:T(8,128)(2,1)} %param.8) | copy-start | bytes 491524
  48.0 52.1 %reduce-scatter.3.cloned.1.call-start = ((), (), s32[]{:S(2)}) async-start(), calls=%async_computation.3 | async-start | bytes 163840 | tf_op jit(solution)/shard_map/reduce_scatter | solution.py:24
  49.3 100.4 %all-gather.2.cloned.1.call-start = ((), (), s32[]{:S(2)}) async-start(), calls=%async_computation.5 | async-start | bytes 1179648 | tf_op jit(solution)/shard_map/all_gather | solution.py:48
  101.5 51.5 %copy-start.1 = (f32[16,4096]{1,0:T(8,128)}, f32[16,4096]{1,0:T(8,128)S(1)}, u32[]{:S(2)}) copy-start(f32[16,4096]{1,0:T(8,128)S(1)} %reshape.26) | copy-start | bytes 786436
  101.5 5.9 %collective-permute-start = (bf16[16,4096]{1,0:T(8,128)(2,1)S(1)}, bf16[16,4096]{1,0:T(8,128)(2,1)S(1)}, u32[]{:S(2)}, u32[]{:S(2)}) collective-permute-start(bf16[16,4096]{1,0:T(8,128)(2,1)S(1)} %convert_element_type.15), channel_id=1, source_target_pairs={{0,1},{1,2},{2,3},{3,0},{4,5},{5,6},{6,7},{7,4},{8,9},{9,10},{10,1... | collective-permute-start | bytes 393224 | tf_op jit(solution)/shard_map/ppermute | solution.py:41
  107.4 5.9 %collective-permute-start.1 = (bf16[16,4096]{1,0:T(8,128)(2,1)S(1)}, bf16[16,4096]{1,0:T(8,128)(2,1)S(1)}, u32[]{:S(2)}, u32[]{:S(2)}) collective-permute-start(bf16[16,4096]{1,0:T(8,128)(2,1)S(1)} %collective-permute-done), channel_id=1, source_target_pairs={{0,1},{1,2},{2,3},{3,0},{4,5},{5,6},{6,7},{7,4},{8,9},{9,10},{10,1... | collective-permute-start | bytes 393224 | tf_op jit(solution)/shard_map/ppermute | solution.py:41
  113.3 5.9 %collective-permute-start.2 = (bf16[16,4096]{1,0:T(8,128)(2,1)S(1)}, bf16[16,4096]{1,0:T(8,128)(2,1)S(1)}, u32[]{:S(2)}, u32[]{:S(2)}) collective-permute-start(bf16[16,4096]{1,0:T(8,128)(2,1)S(1)} %collective-permute-done.1), channel_id=1, source_target_pairs={{0,1},{1,2},{2,3},{3,0},{4,5},{5,6},{6,7},{7,4},{8,9},{9,10},{10,1... | collective-permute-start | bytes 393224 | tf_op jit(solution)/shard_map/ppermute | solution.py:41
Sparse Core Ops, SparseCore 0:
  48.1 24.4 reduce-scatter.4
  75.9 24.1 reduce-scatter.2
  120.2 29.4 all-gather.1
